TPU v7x, 32 devices: a whole 2x2x4 slice. The times are simulated.
32 devices in a mesh: arcs: 2 (over x), trow: 4 (over y, core), tcol: 4 (over z).
Axes of the slice: x: 2, y: 2, z: 4, core: 2. Of those that a mesh axis runs over, the one named last changes fastest.
Arguments:
- design: bfloat16 [1024, 12288], P(('arcs', 'tcol'), 'trow'), may hold values from -6 to 6
- observed: float32 [1024], P(('arcs', 'tcol')), may hold values from -6 to 6
- arc_counts: int32 [32], P(('arcs', 'tcol')), may hold values from 2 to 32
- arc_weight: float32 [32], P(('arcs', 'tcol')), may hold values from 0.3 to 3
Outputs:
- gram: float32 [12288, 12288], P('trow', ('arcs', 'tcol'))
- rhs: float32 [12288], P('trow')
Inputs may be any that keep to these rules, and one draw needn't show every extreme that they name: `arc_counts`: each arc has at least two valid observations.
All inputs are finite; a program needn't handle non-finite values.
Results may differ from a plain program's by a relative error of at most 0.0055.
Values may be sent and summed in bfloat16 or wider, within the bound.
A program may use at most 192 MiB of HBM per device.

v0:
```python
import jax
import jax.numpy as jnp
from jax import lax
from jax.sharding import PartitionSpec as P


def fold_with(right, piece):
    return lax.dot_general(
        piece, right, (((0,), (0,)), ((), ())), preferred_element_type=jnp.float32
    )


def local(design, observed, arc_counts, arc_weight):
    row_count, col_width = design.shape
    arc_total = arc_counts.shape[0]
    arc_len = row_count // arc_total
    slot_index = lax.broadcasted_iota(jnp.int32, (arc_total, arc_len), 1)
    valid_mask = (slot_index < arc_counts[:, None]).astype(jnp.float32)
    counts_float = arc_counts.astype(jnp.float32)
    factor = valid_mask * jnp.sqrt(arc_weight)[:, None]
    blocks = design.reshape(arc_total, arc_len, col_width).astype(jnp.float32)
    column_mean = jnp.sum(valid_mask[:, :, None] * blocks, axis=1) / counts_float[:, None]
    centered = (
        (factor[:, :, None] * (blocks - column_mean[:, None, :]))
        .reshape(row_count, col_width)
        .astype(jnp.bfloat16)
    )
    series = observed.reshape(arc_total, arc_len)
    series_mean = jnp.sum(valid_mask * series, axis=1) / counts_float
    weighted = (factor * (series - series_mean[:, None])).reshape(row_count)
    arc_devices = lax.axis_size("arcs")
    tcol_devices = lax.axis_size("tcol")
    obs_total = row_count * arc_devices * tcol_devices
    rhs_part = jnp.dot(weighted, centered.astype(jnp.float32), precision=lax.Precision.HIGHEST)
    rhs = lax.psum(rhs_part, ("arcs", "tcol")) * obs_total ** (-0.5)
    every_coef = lax.all_gather(centered, "trow", axis=1, tiled=True)
    full_width = every_coef.shape[1]
    narrow = full_width // (arc_devices * tcol_devices)
    shaped = every_coef.reshape(row_count, arc_devices * tcol_devices, narrow)
    moved = lax.all_to_all(shaped, ("arcs", "tcol"), split_axis=1, concat_axis=0, tiled=True)
    right = moved.reshape(row_count * arc_devices * tcol_devices, narrow)
    tile = fold_with(right, lax.all_gather(centered, ("arcs", "tcol"), axis=0, tiled=True))
    gram = tile * (1.0 / obs_total)
    return (gram, rhs)


def solution(mesh):
    return jax.shard_map(
        local,
        mesh=mesh,
        in_specs=(
            P(("arcs", "tcol"), "trow"),
            P(("arcs", "tcol")),
            P(("arcs", "tcol")),
            P(("arcs", "tcol")),
        ),
        out_specs=(P("trow", ("arcs", "tcol")), P("trow")),
        check_vma=False,
    )
```

profile of v0, /device:TPU:0, one launch (start us, length us, event | category | flops | bytes accessed | tf_op | source)
XLA Modules:
  0.0 241.3 jit_solution(7923230437645673761)
XLA Ops:
  7.2 0.0 all-gather.5.cloned.1.call-start
  7.2 0.7 convert_element_type.27
  7.9 0.7 fusion.2
  8.6 0.7 sqrt.3
  9.3 0.7 reshape.91
  10.0 0.8 select_reduce_fusion
  10.8 0.1 mul.48
  10.9 1.5 multiply_reduce_fusion
  12.4 0.1 broadcast_divide_fusion
  12.5 2.2 fusion.1
  14.7 0.0 all-gather.5.cloned.1.call-update
  14.7 0.0 all-gather.3.cloned.1.call-start
  14.8 0.7 all-gather.3.cloned.1.call-update
  15.5 30.6 %all-gather.5.cloned.1.call-done = bf16[128,12288]{1,0:T(8,128)(2,1)} async-done(((bf16[128,3072]{1,0:T(8,128)(2,1)}), bf16[128,12288]{1,0:T(8,128)(2,1)}) %all-gather.5.cloned.1.call-update) | async-done | bytes 3145744 | tf_op jit(solution)/shard_map/all_gather | solution.py:36
  46.1 4.6 %copy.8 = bf16[128,12288]{0,1:T(8,128)(2,1)} copy(bf16[128,12288]{1,0:T(8,128)(2,1)} %all-gather.5.cloned.1.call-done) | data formatting | bytes 6291456 | tf_op jit(solution)/shard_map/all_gather | solution.py:36
  50.7 0.0 copy-start
  50.7 0.0 copy-start.1
  50.7 5.6 %all-to-all-start = ((bf16[128,8,1536]{0,2,1:T(8,128)(2,1)}), bf16[128,8,1536]{0,2,1:T(8,128)(2,1)S(1)}, u32[]{:S(2)}, u32[]{:S(2)}) async-start(bf16[128,8,1536]{0,2,1:T(8,128)(2,1)} %bitcast.21), calls=%async_computation | async-start | bytes 6291456 | tf_op jit(solution)/shard_map/all_to_all | solution.py:40
  56.4 0.0 copy-done
  56.4 0.1 sub.25
  56.5 0.1 sub.26
  56.6 0.0 copy-done.1
  56.6 1.6 fusion.4
  58.1 156.0 %psum.7 = f32[3072]{0:T(1024)S(1)} all-reduce(f32[3072]{0:T(1024)S(1)} %bitcast.23), channel_id=1, replica_groups=mesh['arcs'=2,'trow'=4,'tcol'=4] {'arcs','tcol'}, use_global_device_ids=true, to_apply=%region_2.0 | all-reduce | flops 3072 | bytes 24576 | tf_op jit(solution)/shard_map/psum | solution.py:35
  214.1 0.6 broadcast_multiply_fusion
  214.7 0.0 all-to-all-done
  214.7 2.9 %copy.9 = bf16[8,128,1,1536]{3,1,0,2:T(8,128)(2,1)} copy(bf16[8,128,1,1536]{1,3,0,2:T(8,128)(2,1)S(1)} %bitcast.20) | data formatting | bytes 6291456 | tf_op jit(solution)/shard_map/all_to_all | solution.py:40
  217.6 0.0 all-gather.3.cloned.1.call-done
  217.6 16.8 %convolution_multiply_fusion = f32[3072,1536]{1,0:T(8,128)} fusion(bf16[1024,3072]{1,0:T(8,128)(2,1)} %all-gather.3.cloned.1.call-done, bf16[1024,1536]{1,0:T(8,128)(2,1)} %bitcast.22), kind=kOutput, calls=%fused_computation | convolution fusion | flops 9668395008 | bytes 28311552 | tf_op jit(solution)/shard_map/dot_general | solution.py:8
  (1 shorter events, 0.0 us)
Async XLA Ops:
  7.2 38.9 %all-gather.5.cloned.1.call-start = ((), (), s32[]{:S(2)}) async-start(), calls=%async_computation.2 | async-start | bytes 3932160 | tf_op jit(solution)/shard_map/all_gather | solution.py:36
  14.7 202.9 %all-gather.3.cloned.1.call-start = ((), (), s32[]{:S(2)}) async-start(), calls=%async_computation.1 | async-start | bytes 7077888 | tf_op jit(solution)/shard_map/all_gather | solution.py:42
  50.7 5.6 %copy-start = (s32[4]{0:T(128)S(1)}, s32[4]{0:T(128)}, u32[]{:S(2)}) copy-start(s32[4]{0:T(128)} %param.6) | copy-start | bytes 52
  50.7 5.8 %copy-start.1 = (f32[128]{0:T(128)S(1)}, f32[128]{0:T(128)}, u32[]{:S(2)}) copy-start(f32[128]{0:T(128)} %param.5) | copy-start | bytes 1540
  50.7 164.0 %all-to-all-start = ((bf16[128,8,1536]{0,2,1:T(8,128)(2,1)}), bf16[128,8,1536]{0,2,1:T(8,128)(2,1)S(1)}, u32[]{:S(2)}, u32[]{:S(2)}) async-start(bf16[128,8,1536]{0,2,1:T(8,128)(2,1)} %bitcast.21), calls=%async_computation | async-start | bytes 6291456 | tf_op jit(solution)/shard_map/all_to_all | solution.py:40
Sparse Core Ops, SparseCore 0:
  14.8 31.2 all-gather.4
  48.2 157.1 all-gather.2
where the time goes:
time: 242 us; the launch traced here: 241 us
  blocking collectives  156 us (64%)
  waiting for transfers between devices  31.4 us (13%)
  matrix products  18.4 us (8%)
  between operations  14.1 us (6%)
  local copies, waits for them, and re-layouts  9.13 us (4%)
  other arithmetic  6.6 us (3%)
  starting transfers between devices  5.72 us (2%)
    psum x1, blocking collectives, local(): rhs = lax.psum(rhs_part, ('arcs', 'tcol')) * obs_total ** (-0.5)  156 us
    all_gather x1, waiting for transfers between devices, local(): every_coef = lax.all_gather(centered, 'trow', axis=1, tiled=True)  30.6 us
    dot_general x1, matrix products, fold_with(): lax.dot_general(piece, right, (((0,), (0,)), ((), ())), preferred_element...  16.8 us
    all_to_all x1, starting transfers between devices, local(): lax.all_to_all(shaped, ('arcs', 'tcol'), split_axis=1, concat_axis=0, til...  5.64 us
  transfers between devices with their start and end apart: 3, of which 1 were waited for; matrix products, arithmetic and copies ran while one was open for 4% of the time, Pallas kernels for 0%

commit v1 on v0

--- a/solution.py
+++ b/solution.py
@@ -1,7 +1,13 @@
+import functools
 import jax
 import jax.numpy as jnp
 from jax import lax
+from jax.experimental import pallas as pl
+from jax.experimental.pallas import tpu as pltpu
 from jax.sharding import PartitionSpec as P
+
+MESH = pl.DeviceIdType.MESH
+CHUNKS = 6
 
 
 def fold_with(right, piece):
@@ -10,7 +16,7 @@
     )
 
 
-def local(design, observed, arc_counts, arc_weight):
+def centre(design, observed, arc_counts, arc_weight):
     row_count, col_width = design.shape
     arc_total = arc_counts.shape[0]
     arc_len = row_count // arc_total
@@ -28,6 +34,12 @@
     series = observed.reshape(arc_total, arc_len)
     series_mean = jnp.sum(valid_mask * series, axis=1) / counts_float
     weighted = (factor * (series - series_mean[:, None])).reshape(row_count)
+    return centered, weighted
+
+
+def general(design, observed, arc_counts, arc_weight):
+    centered, weighted = centre(design, observed, arc_counts, arc_weight)
+    row_count = design.shape[0]
     arc_devices = lax.axis_size("arcs")
     tcol_devices = lax.axis_size("tcol")
     obs_total = row_count * arc_devices * tcol_devices
@@ -40,11 +52,324 @@
     moved = lax.all_to_all(shaped, ("arcs", "tcol"), split_axis=1, concat_axis=0, tiled=True)
     right = moved.reshape(row_count * arc_devices * tcol_devices, narrow)
     tile = fold_with(right, lax.all_gather(centered, ("arcs", "tcol"), axis=0, tiled=True))
-    gram = tile * (1.0 / obs_total)
-    return (gram, rhs)
+    return (tile * (1.0 / obs_total), rhs)
+
+
+OWN_X, OWN_UP, OWN_DOWN, TWO_UP, TWO_DOWN, THREE_UP, THREE_DOWN, PAIR_X, TWO_X, REST_X, PAIR_Z = range(11)
+
+
+def kernel(cent, wown, gram, rhs, rows, right, wall, ssem, rsem, osem, qsem, rrsem, wssem, wrsem):
+    n, _, depth, w = cent.shape
+    x, t, z = lax.axis_index("arcs"), lax.axis_index("trow"), lax.axis_index("tcol")
+    y, core = t // 2, t % 2
+    me = x * 4 + z
+    other = (1 - x) * 4
+    obs_total = 8 * depth
+    hz = z % 2
+    pair = z + 1 - 2 * hz
+    two = (z + 2) % 4
+    rest = 3 - z
+    xn = (1 - x, t, z)
+    up = (x, t, jnp.minimum(z + 1, 3))
+    down = (x, t, jnp.maximum(z - 1, 0))
+    mate = (x, t, pair)
+    partner = (x, t + 1 - 2 * core, z)
+    yn = (x, (1 - y) * 2 + core, z)
+    lead = core == z // 2
+    home = y == x
+    is_o = jnp.logical_and(lead, home)
+    is_q = jnp.logical_and(lead, jnp.logical_not(home))
+    not_lead = jnp.logical_not(lead)
+    has_up, has_down = z < 3, z > 0
+    inner = jnp.logical_and(has_up, has_down)
+    outer = jnp.logical_not(inner)
+    low, high = z < 2, z >= 2
+    both = jnp.logical_and
+
+    barrier = pltpu.get_barrier_semaphore()
+    peers = []
+    for dx in range(2):
+        for dz in range(4):
+            if dx or dz:
+                peers.append((dx * 4 + dz, ((x + dx) % 2, t, (z + dz) % 4)))
+    for dev in [p for _, p in peers] + [partner, yn]:
+        pl.semaphore_signal(barrier, inc=1, device_id=dev, device_id_type=MESH)
+    pl.semaphore_wait(barrier, len(peers) + 2)
+
+    def remote(src, dst, send, recv, dev):
+        return pltpu.make_async_remote_copy(
+            src_ref=src, dst_ref=dst, send_sem=send, recv_sem=recv, device_id=dev, device_id_type=MESH
+        )
+
+    def whole(kind, c, s, dev):
+        at = rows.at[c, :, s]
+        return remote(at, at, ssem.at[kind, c], rsem.at[kind, c], dev)
+
+    def half(kind, c, s, h, dev):
+        at = rows.at[c, h, s]
+        return remote(at, at, ssem.at[kind, c], rsem.at[kind, c], dev)
+
+    def own(kind, c, dev):
+        return remote(cent.at[c], rows.at[c, :, me], ssem.at[kind, c], rsem.at[kind, c], dev)
+
+    def right_pair(c, s, src):
+        at = right.at[c, s]
+        return (
+            remote(src, at, osem.at[0, c, s], rrsem.at[c, s], partner),
+            remote(src, at, osem.at[1, c, s], rrsem.at[c, s], yn),
+        )
+
+    def right_out(c, s):
+        @pl.when(is_o)
+        def _():
+            a, b = right_pair(c, s, rows.at[c, hz, s])
+            b.start()
+            a.start()
+
+    def relay_copy(c, s):
+        at = right.at[c, s]
+        return remote(at, at, qsem.at[c, s], rrsem.at[c, s], partner)
+
+    def relay(c, s):
+        @pl.when(is_q)
+        def _():
+            d = relay_copy(c, s)
+            d.wait_recv()
+            d.start()
+
+    def each(body):
+        def step(c, carry):
+            body(c)
+            return carry
+
+        lax.fori_loop(0, n, step, 0)
+
+    def wcopy(k, dev):
+        return remote(wown, wall.at[me], wssem.at[k], wrsem.at[k], dev)
+
+    def phase0(c):
+        own(OWN_X, c, xn).start()
+        pl.when(has_up)(lambda: own(OWN_UP, c, up).start())
+        pl.when(has_down)(lambda: own(OWN_DOWN, c, down).start())
+
+        @pl.when(is_o)
+        def _():
+            a, b = right_pair(c, me, cent.at[c, hz])
+            b.start()
+            a.start()
+
+    each(phase0)
+    for k, dev in peers:
+        wcopy(k, dev).start()
+    wall[me] = wown[...]
+
+    def copy_own(c):
+        rows[c, :, me] = cent[c]
+
+    each(copy_own)
+
+    def phase1(c):
+        @pl.when(has_down)
+        def _():
+            whole(OWN_UP, c, me - 1, up).wait_recv()
+            pl.when(has_up)(lambda: whole(TWO_UP, c, me - 1, up).start())
+
+        @pl.when(has_up)
+        def _():
+            whole(OWN_DOWN, c, me + 1, down).wait_recv()
+            pl.when(has_down)(lambda: whole(TWO_DOWN, c, me + 1, down).start())
+
+        half(PAIR_X, c, x * 4 + pair, hz, xn).start()
+        pl.when(inner)(lambda: whole(REST_X, c, x * 4 + rest, xn).start())
+        right_out(c, x * 4 + pair)
+        pl.when(inner)(lambda: right_out(c, x * 4 + rest))
+        whole(OWN_X, c, other + z, xn).wait_recv()
+        right_out(c, other + z)
+        relay(c, me)
+
+    each(phase1)
+
+    def phase2(c):
+        s = x * 4 + two
+
+        @pl.when(low)
+        def _():
+            whole(TWO_DOWN, c, s, down).wait_recv()
+            pl.when(z == 1)(lambda: whole(THREE_DOWN, c, s, down).start())
+
+        @pl.when(high)
+        def _():
+            whole(TWO_UP, c, s, up).wait_recv()
+            pl.when(z == 2)(lambda: whole(THREE_UP, c, s, up).start())
+
+        whole(TWO_X, c, s, xn).start()
+        right_out(c, s)
+        half(PAIR_X, c, other + pair, hz, xn).wait_recv()
+        right_out(c, other + pair)
+        relay(c, x * 4 + pair)
+        pl.when(inner)(lambda: relay(c, x * 4 + rest))
+        relay(c, other + z)
+
+    each(phase2)
+    each(lambda c: half(PAIR_Z, c, other + z, hz, mate).start())
+
+    def phase3(c):
+        @pl.when(outer)
+        def _():
+            s = x * 4 + rest
+            pl.when(z == 0)(lambda: whole(THREE_DOWN, c, s, down).wait_recv())
+            pl.when(z == 3)(lambda: whole(THREE_UP, c, s, up).wait_recv())
+            whole(REST_X, c, s, xn).start()
+            right_out(c, s)
+
+        whole(TWO_X, c, other + two, xn).wait_recv()
+        right_out(c, other + two)
+        relay(c, x * 4 + two)
+        relay(c, other + pair)
+
+    each(phase3)
+
+    for k, dev in peers:
+        wcopy(k, dev).wait_recv()
+    wide = jnp.concatenate([wall[s] for s in range(8)], axis=1)
+    hi = wide.astype(jnp.bfloat16).astype(jnp.float32)
+    mid = (wide - hi).astype(jnp.bfloat16).astype(jnp.float32)
+    low_part = wide - hi - mid
+    pick = lax.broadcasted_iota(jnp.int32, wide.shape, 0)
+    terms = jnp.where(pick == 0, hi, jnp.where(pick == 1, mid, jnp.where(pick == 2, low_part, 0.0)))
+    terms = terms.astype(jnp.bfloat16)
+
+    def tile(c1, c2):
+        b = right[c2].reshape(obs_total, w)
+        for h in range(2):
+            a = rows[c1, h].reshape(obs_total, w)
+            gram[pl.ds(pl.multiple_of(h * n * w + c1 * w, w), w), pl.ds(pl.multiple_of(c2 * w, w), w)] = fold_with(
+                b, a
+            ) * (1.0 / obs_total)
+
+    def finish(c):
+        relay(c, other + rest)
+
+        @pl.when(not_lead)
+        def _():
+            for s in range(8):
+                relay_copy(c, s).wait_recv()
+
+        @pl.when(is_o)
+        def _():
+            right[c] = rows[c, hz]
+
+        for h in range(2):
+            a = rows[c, h].reshape(obs_total, w)
+            part = lax.dot_general(terms, a, (((1,), (0,)), ((), ())), preferred_element_type=jnp.float32)
+            rhs[pl.ds(h * n + c, 1), :] = jnp.sum(part, axis=0, keepdims=True) * obs_total ** (-0.5)
+
+        def step(k, carry):
+            tile(c, k)
+            tile(k, c)
+            return carry
+
+        lax.fori_loop(0, c, step, 0)
+        tile(c, c)
+
+    def phase4(c):
+        whole(REST_X, c, other + rest, xn).wait_recv()
+        right_out(c, other + rest)
+
+        @pl.when(outer)
+        def _():
+            s = x * 4 + rest
+            relay(c, s)
+
+        relay(c, other + two)
+        half(PAIR_Z, c, other + pair, 1 - hz, mate).wait_recv()
+        pl.when(c > 0)(lambda: finish(c - 1))
+
+    each(phase4)
+    finish(n - 1)
+
+    def drain(c):
+        own(OWN_X, c, xn).wait_send()
+        pl.when(has_up)(lambda: own(OWN_UP, c, up).wait_send())
+        pl.when(has_down)(lambda: own(OWN_DOWN, c, down).wait_send())
+
+        @pl.when(inner)
+        def _():
+            whole(TWO_UP, c, me - 1, up).wait_send()
+            whole(TWO_DOWN, c, me + 1, down).wait_send()
+
+        pl.when(z == 1)(lambda: whole(THREE_DOWN, c, me, down).wait_send())
+        pl.when(z == 2)(lambda: whole(THREE_UP, c, me, up).wait_send())
+        half(PAIR_X, c, me, hz, xn).wait_send()
+        whole(TWO_X, c, me, xn).wait_send()
+        whole(REST_X, c, me, xn).wait_send()
+        half(PAIR_Z, c, me, hz, mate).wait_send()
+
+        def pieces(s, carry):
+            @pl.when(is_o)
+            def _():
+                a, b = right_pair(c, s, rows.at[c, hz, s])
+                a.wait_send()
+                b.wait_send()
+
+            pl.when(is_q)(lambda: relay_copy(c, s).wait_send())
+            return carry
+
+        lax.fori_loop(0, 8, pieces, 0)
+
+    each(drain)
+    for k, dev in peers:
+        wcopy(k, dev).wait_send()
+
+
+def gathered(design, observed, arc_counts, arc_weight):
+    centered, weighted = centre(design, observed, arc_counts, arc_weight)
+    depth, width = design.shape
+    n = CHUNKS
+    w = width // (2 * n)
+    cent = centered.reshape(depth, 2, n, w).transpose(2, 1, 0, 3)
+    wown = jnp.broadcast_to(weighted[None, :], (8, depth))
+    vmem = pl.BlockSpec(memory_space=pltpu.VMEM)
+    dma = pltpu.SemaphoreType.DMA
+    gram, rhs = pl.pallas_call(
+        kernel,
+        out_shape=(
+            pltpu.VMEM((width, n * w), jnp.float32) if IN_VMEM else jax.ShapeDtypeStruct((width, n * w), jnp.float32),
+            jax.ShapeDtypeStruct((2 * n, w), jnp.float32),
+        ),
+        in_specs=[vmem, vmem],
+        out_specs=(vmem, vmem),
+        scratch_shapes=[
+            pltpu.VMEM((n, 2, 8, depth, w), jnp.bfloat16),
+            pltpu.VMEM((n, 8, depth, w), jnp.bfloat16),
+            pltpu.VMEM((8, 8, depth), jnp.float32),
+            dma((11, n)),
+            dma((11, n)),
+            dma((2, n, 8)),
+            dma((n, 8)),
+            dma((n, 8)),
+            dma((8,)),
+            dma((8,)),
+        ],
+        compiler_params=pltpu.CompilerParams(
+            collective_id=0, has_side_effects=True, vmem_limit_bytes=VMEM_LIMIT
+        ),
+    )(cent, wown)
+    return gram, rhs.reshape(width)
+
+
+IN_VMEM = True
+VMEM_LIMIT = 40 * 1024 * 1024
 
 
 def solution(mesh):
+    sizes = (mesh.shape["arcs"], mesh.shape["trow"], mesh.shape["tcol"])
+
+    def local(design, observed, arc_counts, arc_weight):
+        fits = sizes == (2, 4, 4) and design.shape[0] == 128 and design.shape[1] % (2 * CHUNKS * 128) == 0
+        body = gathered if fits else general
+        return body(design, observed, arc_counts, arc_weight)
+
     return jax.shard_map(
         local,
         mesh=mesh,

time: 242 us -> 110 us (0.45)
  the two profiles are of different devices: /device:TPU:0 before, /device:TPU:11 now
where the time goes in v1:
time: 110 us; the launch traced here: 109 us
  Pallas kernels  91.1 us (83%)
  local copies, waits for them, and re-layouts  11.2 us (10%)
  other arithmetic  6.43 us (6%)
    pallas_call x1, Pallas kernels, gathered(): pl.pallas_call(kernel, out_shape=(pltpu.VMEM((width, n * w), jnp.float32)...  91.1 us
    unnamed x3, local copies, waits for them, and re-layouts  6.86 us

profile of v1, /device:TPU:11, one launch (start us, length us, event | category | flops | bytes accessed | tf_op | source)
XLA Modules:
  0.0 109.5 jit_solution(12672294190773005331)
XLA Ops:
  0.6 0.7 sqrt.3
  1.3 0.7 convert_element_type.26
  2.0 0.7 reshape.106
  2.7 0.8 select_reduce_fusion
  3.5 0.7 convert_divide_fusion
  4.2 0.1 mul.37
  4.3 0.1 sub.26
  4.3 0.1 sub.27
  4.4 0.7 subtract_multiply_fusion
  5.1 0.7 fusion.2
  5.8 0.6 broadcast_in_dim.2.wown
  6.4 1.4 %multiply_reduce_fusion = f32[4,3072]{1,0:T(4,128)S(1)} fusion(f32[4,32]{1,0:T(4,128)S(1)} %fusion.2, bf16[128,3072]{1,0:T(8,128)(2,1)} %param.4), kind=kLoop, calls=%fused_computation.3 | loop fusion | flops 1167360 | bytes 836096 | tf_op jit(solution)/shard_map/reduce_sum | solution.py:28
  7.9 0.1 broadcast_divide_fusion
  7.9 1.4 %fusion.1 = bf16[128,3072]{1,0:T(8,128)(2,1)S(1)} fusion(f32[4,3072]{1,0:T(4,128)S(1)} %broadcast_divide_fusion, f32[128]{0:T(128)S(1)} %mul.37, bf16[128,3072]{1,0:T(8,128)(2,1)} %param.4), kind=kLoop, calls=%fused_computation.2 | loop fusion | flops 1572864 | bytes 1622528 | tf_op jit(solution)/shard_map/convert_element_type | solution.py:32
  9.3 0.4 copy.8
  9.7 1.2 %copy.9 = bf16[128,2,6,256]{3,0,1,2:T(8,128)(2,1)} copy(bf16[128,2,6,256]{0,3,2,1:T(8,128)(2,1)S(1)} %bitcast.11) | data formatting | bytes 1572864 | tf_op jit(solution)/shard_map/reshape | solution.py:330
  10.8 91.1 %shard_map.59 = (f32[3072,1536]{1,0:T(8,128)S(1)}, f32[12,256]{1,0:T(8,128)}) custom-call(bf16[6,2,128,256]{3,2,1,0:T(8,128)(2,1)} %bitcast.10, f32[8,128]{1,0:T(8,128)} %broadcast_in_dim.2.wown), custom_call_target="tpu_custom_call" | custom-call | tf_op jit(solution)/shard_map/pallas_call | solution.py:334
  102.0 0.0 copy-start
  102.0 6.9 %copy.11 = f32[3072,1536]{1,0:T(8,128)} copy(f32[3072,1536]{1,0:T(8,128)S(1)} %get-tuple-element.8) | data formatting | bytes 37748736
  108.8 0.0 copy-done
  108.8 0.6 reshape.107
Async XLA Ops:
  102.0 6.9 %copy-start = (f32[12,256]{1,0:T(8,128)S(1)}, f32[12,256]{1,0:T(8,128)}, u32[]{:S(2)}) copy-start(f32[12,256]{1,0:T(8,128)} %get-tuple-element.5) | copy-start | bytes 36868

commit v2 on v1

--- a/solution.py
+++ b/solution.py
@@ -58,8 +58,13 @@
 OWN_X, OWN_UP, OWN_DOWN, TWO_UP, TWO_DOWN, THREE_UP, THREE_DOWN, PAIR_X, TWO_X, REST_X, PAIR_Z = range(11)
 
 
-def kernel(cent, wown, gram, rhs, rows, right, wall, ssem, rsem, osem, qsem, rrsem, wssem, wrsem):
-    n, _, depth, w = cent.shape
+def kernel(
+    design, series, counts, weights, gram, rhs, rows, right, flipped, ready, wown, wall, share, scale,
+    ssem, rsem, osem, qsem, rrsem, wssem, wrsem,
+):
+    n, _, _, depth, w = rows.shape
+    arcs_here = counts.shape[0]
+    arc_len = depth // arcs_here
     x, t, z = lax.axis_index("arcs"), lax.axis_index("trow"), lax.axis_index("tcol")
     y, core = t // 2, t % 2
     me = x * 4 + z
@@ -79,12 +84,10 @@
     home = y == x
     is_o = jnp.logical_and(lead, home)
     is_q = jnp.logical_and(lead, jnp.logical_not(home))
-    not_lead = jnp.logical_not(lead)
     has_up, has_down = z < 3, z > 0
     inner = jnp.logical_and(has_up, has_down)
     outer = jnp.logical_not(inner)
     low, high = z < 2, z >= 2
-    both = jnp.logical_and
 
     barrier = pltpu.get_barrier_semaphore()
     peers = []
@@ -94,6 +97,26 @@
                 peers.append((dx * 4 + dz, ((x + dx) % 2, t, (z + dz) % 4)))
     for dev in [p for _, p in peers] + [partner, yn]:
         pl.semaphore_signal(barrier, inc=1, device_id=dev, device_id_type=MESH)
+
+    lane = lax.broadcasted_iota(jnp.int32, (8, depth), 1)
+    arc = lane // arc_len
+    count = jnp.full((8, depth), 1, jnp.int32)
+    weight = jnp.zeros((8, depth), jnp.float32)
+    for a in range(arcs_here):
+        count = jnp.where(arc == a, counts[a], count)
+        weight = jnp.where(arc == a, weights[a], weight)
+    valid = (lane - arc * arc_len < count).astype(jnp.float32)
+    portion = valid / count.astype(jnp.float32)
+    factor = valid * jnp.sqrt(weight)
+    line = jnp.broadcast_to(series[...], (8, depth))
+    average = jnp.zeros((8, depth), jnp.float32)
+    for a in range(arcs_here):
+        total = jnp.sum(jnp.where(arc == a, valid * line, 0.0), axis=1, keepdims=True)
+        average = jnp.where(arc == a, total / count.astype(jnp.float32), average)
+    weighted = factor * (line - average)
+    level = lax.broadcasted_iota(jnp.int32, (8, depth), 0)
+    wown[...] = jnp.where(level == 0, weighted, jnp.where(level == 1, portion, factor))
+    wall[me] = wown[...]
     pl.semaphore_wait(barrier, len(peers) + 2)
 
     def remote(src, dst, send, recv, dev):
@@ -109,8 +132,12 @@
         at = rows.at[c, h, s]
         return remote(at, at, ssem.at[kind, c], rsem.at[kind, c], dev)
 
+    def mine(c, h):
+        return design.at[:, pl.ds(pl.multiple_of((h * n + c) * w, w), w)]
+
     def own(kind, c, dev):
-        return remote(cent.at[c], rows.at[c, :, me], ssem.at[kind, c], rsem.at[kind, c], dev)
+        for h in range(2):
+            remote(mine(c, h), rows.at[c, h, me], ssem.at[kind, c], rsem.at[kind, c], dev).start()
 
     def right_pair(c, s, src):
         at = right.at[c, s]
@@ -130,12 +157,30 @@
         at = right.at[c, s]
         return remote(at, at, qsem.at[c, s], rrsem.at[c, s], partner)
 
+    def centre_block(block, s):
+        wide = block.astype(jnp.float32).reshape(arcs_here, arc_len, w)
+        part = jnp.concatenate([share[s]] * (w // 128), axis=1).reshape(arcs_here, arc_len, w)
+        gain = jnp.concatenate([scale[s]] * (w // 128), axis=1).reshape(arcs_here, arc_len, w)
+        mean = jnp.sum(part * wide, axis=1, keepdims=True)
+        return (gain * (wide - mean)).reshape(depth, w).astype(jnp.bfloat16)
+
+    def take(c, s):
+        for h in range(2):
+            flipped[c, pl.ds(h * w, w), pl.ds(pl.multiple_of(s * depth, depth), depth)] = centre_block(
+                rows[c, h, s], s
+            ).T
+
     def relay(c, s):
-        @pl.when(is_q)
+        @pl.when(jnp.logical_not(is_o))
         def _():
             d = relay_copy(c, s)
             d.wait_recv()
-            d.start()
+            pl.when(is_q)(d.start)
+            ready[c, pl.ds(pl.multiple_of(s * depth, depth), depth), :] = centre_block(right[c, s], s)
+
+        @pl.when(is_o)
+        def _():
+            ready[c, pl.ds(pl.multiple_of(s * depth, depth), depth), :] = centre_block(rows[c, hz, s], s)
 
     def each(body):
         def step(c, carry):
@@ -148,25 +193,36 @@
         return remote(wown, wall.at[me], wssem.at[k], wrsem.at[k], dev)
 
     def phase0(c):
-        own(OWN_X, c, xn).start()
-        pl.when(has_up)(lambda: own(OWN_UP, c, up).start())
-        pl.when(has_down)(lambda: own(OWN_DOWN, c, down).start())
+        own(OWN_X, c, xn)
+        pl.when(has_up)(lambda: own(OWN_UP, c, up))
+        pl.when(has_down)(lambda: own(OWN_DOWN, c, down))
 
         @pl.when(is_o)
         def _():
-            a, b = right_pair(c, me, cent.at[c, hz])
+            a, b = right_pair(c, me, mine(c, hz))
             b.start()
             a.start()
 
-    each(phase0)
     for k, dev in peers:
         wcopy(k, dev).start()
-    wall[me] = wown[...]
+    each(phase0)
 
     def copy_own(c):
-        rows[c, :, me] = cent[c]
+        for h in range(2):
+            rows[c, h, me] = design[:, pl.ds(pl.multiple_of((h * n + c) * w, w), w)]
 
     each(copy_own)
+    for k, dev in peers:
+        wcopy(k, dev).wait_recv()
+
+    def spread(s, carry):
+        columns = wall[s].T
+        share[s] = jnp.broadcast_to(columns[:, 1:2], (depth, 128))
+        scale[s] = jnp.broadcast_to(columns[:, 2:3], (depth, 128))
+        return carry
+
+    lax.fori_loop(0, 8, spread, 0)
+    each(lambda c: take(c, me))
 
     def phase1(c):
         @pl.when(has_down)
@@ -185,6 +241,9 @@
         pl.when(inner)(lambda: right_out(c, x * 4 + rest))
         whole(OWN_X, c, other + z, xn).wait_recv()
         right_out(c, other + z)
+        take(c, x * 4 + pair)
+        pl.when(inner)(lambda: take(c, x * 4 + rest))
+        take(c, other + z)
         relay(c, me)
 
     each(phase1)
@@ -206,6 +265,7 @@
         right_out(c, s)
         half(PAIR_X, c, other + pair, hz, xn).wait_recv()
         right_out(c, other + pair)
+        take(c, s)
         relay(c, x * 4 + pair)
         pl.when(inner)(lambda: relay(c, x * 4 + rest))
         relay(c, other + z)
@@ -221,17 +281,17 @@
             pl.when(z == 3)(lambda: whole(THREE_UP, c, s, up).wait_recv())
             whole(REST_X, c, s, xn).start()
             right_out(c, s)
+            take(c, s)
 
         whole(TWO_X, c, other + two, xn).wait_recv()
         right_out(c, other + two)
+        take(c, other + two)
         relay(c, x * 4 + two)
         relay(c, other + pair)
 
     each(phase3)
 
-    for k, dev in peers:
-        wcopy(k, dev).wait_recv()
-    wide = jnp.concatenate([wall[s] for s in range(8)], axis=1)
+    wide = jnp.concatenate([jnp.broadcast_to(wall[s][0:1], (8, depth)) for s in range(8)], axis=1)
     hi = wide.astype(jnp.bfloat16).astype(jnp.float32)
     mid = (wide - hi).astype(jnp.bfloat16).astype(jnp.float32)
     low_part = wide - hi - mid
@@ -240,29 +300,20 @@
     terms = terms.astype(jnp.bfloat16)
 
     def tile(c1, c2):
-        b = right[c2].reshape(obs_total, w)
+        both_parts = lax.dot_general(
+            flipped[c1], ready[c2], (((1,), (0,)), ((), ())), preferred_element_type=jnp.float32
+        ) * (1.0 / obs_total)
         for h in range(2):
-            a = rows[c1, h].reshape(obs_total, w)
-            gram[pl.ds(pl.multiple_of(h * n * w + c1 * w, w), w), pl.ds(pl.multiple_of(c2 * w, w), w)] = fold_with(
-                b, a
-            ) * (1.0 / obs_total)
+            gram[
+                pl.ds(pl.multiple_of(h * n * w + c1 * w, w), w), pl.ds(pl.multiple_of(c2 * w, w), w)
+            ] = both_parts[h * w : (h + 1) * w]
 
     def finish(c):
         relay(c, other + rest)
-
-        @pl.when(not_lead)
-        def _():
-            for s in range(8):
-                relay_copy(c, s).wait_recv()
-
-        @pl.when(is_o)
-        def _():
-            right[c] = rows[c, hz]
-
+        part = lax.dot_general(terms, flipped[c], (((1,), (1,)), ((), ())), preferred_element_type=jnp.float32)
+        total = jnp.sum(part, axis=0, keepdims=True) * obs_total ** (-0.5)
         for h in range(2):
-            a = rows[c, h].reshape(obs_total, w)
-            part = lax.dot_general(terms, a, (((1,), (0,)), ((), ())), preferred_element_type=jnp.float32)
-            rhs[pl.ds(h * n + c, 1), :] = jnp.sum(part, axis=0, keepdims=True) * obs_total ** (-0.5)
+            rhs[pl.ds(h * n + c, 1), :] = total[:, h * w : (h + 1) * w]
 
         def step(k, carry):
             tile(c, k)
@@ -283,15 +334,17 @@
 
         relay(c, other + two)
         half(PAIR_Z, c, other + pair, 1 - hz, mate).wait_recv()
+        take(c, other + pair)
+        take(c, other + rest)
         pl.when(c > 0)(lambda: finish(c - 1))
 
     each(phase4)
     finish(n - 1)
 
     def drain(c):
-        own(OWN_X, c, xn).wait_send()
-        pl.when(has_up)(lambda: own(OWN_UP, c, up).wait_send())
-        pl.when(has_down)(lambda: own(OWN_DOWN, c, down).wait_send())
+        whole(OWN_X, c, me, xn).wait_send()
+        pl.when(has_up)(lambda: whole(OWN_UP, c, me, up).wait_send())
+        pl.when(has_down)(lambda: whole(OWN_DOWN, c, me, down).wait_send())
 
         @pl.when(inner)
         def _():
@@ -323,13 +376,11 @@
 
 
 def gathered(design, observed, arc_counts, arc_weight):
-    centered, weighted = centre(design, observed, arc_counts, arc_weight)
     depth, width = design.shape
     n = CHUNKS
     w = width // (2 * n)
-    cent = centered.reshape(depth, 2, n, w).transpose(2, 1, 0, 3)
-    wown = jnp.broadcast_to(weighted[None, :], (8, depth))
     vmem = pl.BlockSpec(memory_space=pltpu.VMEM)
+    smem = pl.BlockSpec(memory_space=pltpu.SMEM)
     dma = pltpu.SemaphoreType.DMA
     gram, rhs = pl.pallas_call(
         kernel,
@@ -337,12 +388,17 @@
             pltpu.VMEM((width, n * w), jnp.float32) if IN_VMEM else jax.ShapeDtypeStruct((width, n * w), jnp.float32),
             jax.ShapeDtypeStruct((2 * n, w), jnp.float32),
         ),
-        in_specs=[vmem, vmem],
+        in_specs=[vmem, vmem, smem, smem],
         out_specs=(vmem, vmem),
         scratch_shapes=[
             pltpu.VMEM((n, 2, 8, depth, w), jnp.bfloat16),
             pltpu.VMEM((n, 8, depth, w), jnp.bfloat16),
+            pltpu.VMEM((n, 2 * w, 8 * depth), jnp.bfloat16),
+            pltpu.VMEM((n, 8 * depth, w), jnp.bfloat16),
+            pltpu.VMEM((8, depth), jnp.float32),
             pltpu.VMEM((8, 8, depth), jnp.float32),
+            pltpu.VMEM((8, depth, 128), jnp.float32),
+            pltpu.VMEM((8, depth, 128), jnp.float32),
             dma((11, n)),
             dma((11, n)),
             dma((2, n, 8)),
@@ -354,7 +410,7 @@
         compiler_params=pltpu.CompilerParams(
             collective_id=0, has_side_effects=True, vmem_limit_bytes=VMEM_LIMIT
         ),
-    )(cent, wown)
+    )(design, observed[None, :], arc_counts, arc_weight)
     return gram, rhs.reshape(width)
 
 

time: 110 us -> 101 us (0.918)
  other arithmetic: 6.43 us -> 0 us
  local copies, waits for them, and re-layouts: 11.2 us -> 7.46 us
  Pallas kernels: 91.1 us -> 92.9 us
    convert_element_type x3 -> x0, other arithmetic: 2.74 us -> none  [the longest x1 1.35 us: centre(): centered = (factor[:, :, None] * (blocks - column_mean[:, None, :])).resh...]
    reduce_sum x2 -> x0, other arithmetic: 2.29 us -> none  [the longest x1 1.45 us: centre(): jnp.sum(valid_mask[:, :, None] * blocks, axis=1) / counts_float[:, None]]
    reshape x2 -> x0, local copies, waits for them, and re-layouts: 1.9 us -> none  [the longest x1 1.17 us: gathered(): cent = centered.reshape(depth, 2, n, w).transpose(2, 1, 0, 3)]
    pallas_call x1, Pallas kernels: 91.1 us -> 92.9 us  [gathered(): pl.pallas_call(kernel, out_shape=(pltpu.VMEM((width, n * w), jnp.float32)...]
where the time goes in v2:
time: 101 us
  Pallas kernels  92.9 us (92%)
  local copies, waits for them, and re-layouts  7.46 us (7%)
    pallas_call x1, Pallas kernels, gathered(): pl.pallas_call(kernel, out_shape=(pltpu.VMEM((width, n * w), jnp.float32)...  92.9 us
    unnamed x3, local copies, waits for them, and re-layouts  6.86 us

profile of v2, /device:TPU:11, one launch (start us, length us, event | category | flops | bytes accessed | tf_op | source)
XLA Modules:
  0.0 101.0 jit_solution(6065124907492518849)
XLA Ops:
  0.6 92.9 %shard_map.59 = (f32[3072,1536]{1,0:T(8,128)S(1)}, f32[12,256]{1,0:T(8,128)}) custom-call(bf16[128,3072]{1,0:T(8,128)(2,1)} %design.1, f32[1,128]{1,0:T(1,128)} %bitcast.1, s32[4]{0:T(128)} %counts.1, f32[4]{0:T(128)} %weights.1), custom_call_target="tpu_custom_call" | custom-call | tf_op jit(solution)/shard_map/pallas_call | solution.py:385
  93.6 0.0 copy-start
  93.6 6.9 %copy.7 = f32[3072,1536]{1,0:T(8,128)} copy(f32[3072,1536]{1,0:T(8,128)S(1)} %get-tuple-element.6) | data formatting | bytes 37748736
  100.4 0.0 copy-done
  100.4 0.6 reshape.7
Async XLA Ops:
  93.6 6.9 %copy-start = (f32[12,256]{1,0:T(8,128)S(1)}, f32[12,256]{1,0:T(8,128)}, u32[]{:S(2)}) copy-start(f32[12,256]{1,0:T(8,128)} %get-tuple-element.5) | copy-start | bytes 36868

commit v3 on v2

--- a/solution.py
+++ b/solution.py
@@ -88,6 +88,10 @@
     inner = jnp.logical_and(has_up, has_down)
     outer = jnp.logical_not(inner)
     low, high = z < 2, z >= 2
+    early_kind = jnp.where(outer, TWO_X, REST_X)
+    late_kind = jnp.where(outer, REST_X, TWO_X)
+    early = other + jnp.where(outer, two, rest)
+    late = other + jnp.where(outer, rest, two)
 
     barrier = pltpu.get_barrier_semaphore()
     peers = []
@@ -283,9 +287,9 @@
             right_out(c, s)
             take(c, s)
 
-        whole(TWO_X, c, other + two, xn).wait_recv()
-        right_out(c, other + two)
-        take(c, other + two)
+        whole(early_kind, c, early, xn).wait_recv()
+        right_out(c, early)
+        take(c, early)
         relay(c, x * 4 + two)
         relay(c, other + pair)
 
@@ -309,7 +313,7 @@
             ] = both_parts[h * w : (h + 1) * w]
 
     def finish(c):
-        relay(c, other + rest)
+        relay(c, late)
         part = lax.dot_general(terms, flipped[c], (((1,), (1,)), ((), ())), preferred_element_type=jnp.float32)
         total = jnp.sum(part, axis=0, keepdims=True) * obs_total ** (-0.5)
         for h in range(2):
@@ -324,18 +328,18 @@
         tile(c, c)
 
     def phase4(c):
-        whole(REST_X, c, other + rest, xn).wait_recv()
-        right_out(c, other + rest)
+        whole(late_kind, c, late, xn).wait_recv()
+        right_out(c, late)
 
         @pl.when(outer)
         def _():
             s = x * 4 + rest
             relay(c, s)
 
-        relay(c, other + two)
+        relay(c, early)
         half(PAIR_Z, c, other + pair, 1 - hz, mate).wait_recv()
         take(c, other + pair)
-        take(c, other + rest)
+        take(c, late)
         pl.when(c > 0)(lambda: finish(c - 1))
 
     each(phase4)

time: 101 us -> 94.9 us (0.940)
  the two profiles are of different devices: /device:TPU:11 before, /device:TPU:3 now
where the time goes in v3:
time: 94.9 us; the launch traced here: 94.7 us
  Pallas kernels  86.6 us (91%)
  local copies, waits for them, and re-layouts  7.46 us (8%)
    pallas_call x1, Pallas kernels, gathered(): pl.pallas_call(kernel, out_shape=(pltpu.VMEM((width, n * w), jnp.float32)...  86.6 us
    unnamed x3, local copies, waits for them, and re-layouts  6.86 us

profile of v3, /device:TPU:3, one launch (start us, length us, event | category | flops | bytes accessed | tf_op | source)
XLA Modules:
  0.0 94.7 jit_solution(3485139955827205565)
XLA Ops:
  0.6 86.6 %shard_map.59 = (f32[3072,1536]{1,0:T(8,128)S(1)}, f32[12,256]{1,0:T(8,128)}) custom-call(bf16[128,3072]{1,0:T(8,128)(2,1)} %design.1, f32[1,128]{1,0:T(1,128)} %bitcast.1, s32[4]{0:T(128)} %counts.1, f32[4]{0:T(128)} %weights.1), custom_call_target="tpu_custom_call" | custom-call | tf_op jit(solution)/shard_map/pallas_call | solution.py:389
  87.3 0.0 copy-start
  87.3 6.9 %copy.7 = f32[3072,1536]{1,0:T(8,128)} copy(f32[3072,1536]{1,0:T(8,128)S(1)} %get-tuple-element.6) | data formatting | bytes 37748736
  94.1 0.0 copy-done
  94.1 0.6 reshape.7
Async XLA Ops:
  87.3 6.9 %copy-start = (f32[12,256]{1,0:T(8,128)S(1)}, f32[12,256]{1,0:T(8,128)}, u32[]{:S(2)}) copy-start(f32[12,256]{1,0:T(8,128)} %get-tuple-element.5) | copy-start | bytes 36868
